TPU v7x, 32 devices: a whole 2x2x4 slice. The times are simulated.
32 devices in a mesh: group: 8 (over z, y), rep: 4 (over x, core).
Axes of the slice: x: 2, y: 2, z: 4, core: 2. Of those that a mesh axis runs over, the one named last changes fastest.
Arguments:
- grad_parts: bfloat16 [4, 24, 1024, 1024], P('rep', None, 'group'), may hold values from -40 to 40
- params: bfloat16 [24, 1024, 1024], P('rep', 'group'), may hold values from -6 to 6
- accum: float32 [24, 1024, 1024], P('rep', 'group'), may hold values from 1 to 50
- left_pre: bfloat16 [4, 8, 1, 1024, 1024], P('rep', 'group'), may hold values from -1 to 4
- right_pre: bfloat16 [4, 8, 1, 1024, 1024], P('rep', 'group'), may hold values from -1 to 4
- slot_block: int32 [4, 8, 1], replicated, may hold values from -1 to 5, as said below
- layer_of: int32 [24], replicated, may hold values from 0 to 7
Outputs:
- new_params: bfloat16 [24, 1024, 1024], P(None, 'group')
- new_accum: float32 [24, 1024, 1024], P('rep', 'group')
Inputs may be any that keep to these rules, and one draw needn't show every extreme that they name: For every replica q each of its 6 blocks is named by exactly one slot of slot_block[q]; a device's used slots come first and the others hold -1; in every replica some device has all 1 slots used.
All inputs are finite; a program needn't handle non-finite values.
Results may differ from a plain program's by a relative error of at most 0.018.
Values may be sent and summed in bfloat16 or wider, within the bound.
A program may use at most 128 MiB of HBM per device.

v0:
```python
import jax
import jax.numpy as jnp
from jax import lax
from jax.sharding import PartitionSpec as P

LAYERS = 8


step_rate = 0.5


def send_back(precond, group_size):
    slot_count = precond.shape[0]
    block_width = precond.shape[2]
    shard_rows = block_width // group_size
    spread = precond.reshape(1, slot_count, group_size, shard_rows, block_width)
    returned = lax.all_to_all(spread, "group", split_axis=2, concat_axis=0, tiled=True)
    return returned.reshape(group_size * slot_count, shard_rows, block_width)


def local(grad_parts, params, accum, left_pre, right_pre, slot_block, layer_of):
    group_size = lax.axis_size("group")
    replica_index = lax.axis_index("rep")
    group_index = lax.axis_index("group")
    blocks_rep = params.shape[0]
    shard_rows = params.shape[1]
    block_width = params.shape[2]
    slot_count = left_pre.shape[2]
    summed = lax.psum_scatter(
        grad_parts[0].astype(jnp.float32).astype(jnp.bfloat16),
        "rep",
        scatter_dimension=0,
        tiled=True,
    )
    gradient_wide = summed.astype(jnp.float32)
    new_accum = accum + gradient_wide * gradient_wide
    graft = gradient_wide * lax.rsqrt(new_accum)
    graft_blocks = jnp.sum(graft * graft, axis=(1, 2))
    my_layers = lax.dynamic_slice_in_dim(layer_of, replica_index * blocks_rep, blocks_rep)
    onehot_rep = (my_layers[:, None] == jnp.arange(LAYERS, dtype=jnp.int32)[None, :]).astype(
        jnp.float32
    )
    graft_layer = jnp.sum(onehot_rep * graft_blocks[:, None], axis=0)
    owner_table = lax.dynamic_index_in_dim(slot_block, replica_index, 0, keepdims=False)
    flat_table = owner_table.reshape(-1)
    slot_valid = flat_table >= 0
    picked = jnp.take(summed, jnp.maximum(flat_table, 0), axis=0)
    outgoing = jnp.where(slot_valid[:, None, None], picked, jnp.zeros_like(picked))
    outgoing = outgoing.reshape(group_size, slot_count, shard_rows, block_width)
    owned_blocks = lax.all_to_all(outgoing, "group", split_axis=0, concat_axis=2, tiled=True)[0]
    lefts = left_pre[0, 0]
    rights = right_pre[0, 0]
    left_product = jnp.einsum(
        "sij,sjk->sik", lefts, owned_blocks, preferred_element_type=jnp.float32
    ).astype(jnp.bfloat16)
    precond = jnp.einsum(
        "sij,sjk->sik", left_product, rights, preferred_element_type=jnp.float32
    ).astype(jnp.bfloat16)
    slot_total = flat_table.shape[0]
    position = jnp.sum(
        jnp.where(
            flat_table[None, :] == jnp.arange(blocks_rep, dtype=jnp.int32)[:, None],
            jnp.arange(slot_total, dtype=jnp.int32)[None, :],
            0,
        ),
        axis=1,
    )
    precond_wide = precond.astype(jnp.float32)
    slot_squares = jnp.sum(precond_wide * precond_wide, axis=(1, 2))
    my_slots = lax.dynamic_index_in_dim(owner_table, group_index, 0, keepdims=False)
    selected = (my_slots[:, None] == jnp.arange(blocks_rep, dtype=jnp.int32)[None, :]).astype(
        jnp.float32
    )
    slot_onehot = jnp.sum(selected[:, :, None] * onehot_rep[None, :, :], axis=1)
    shampoo_part = jnp.sum(slot_onehot * slot_squares[:, None], axis=0)
    graft_sq, shampoo_sq = lax.psum((graft_layer, shampoo_part), ("group", "rep"))
    returned = send_back(precond, group_size)
    precond_rows = jnp.take(returned, position, axis=0)
    layer_scale = jnp.sqrt(graft_sq) * lax.rsqrt(shampoo_sq + 1e-06)
    block_scale = jnp.sum(onehot_rep * layer_scale[None, :], axis=1)
    updated = (
        params.astype(jnp.float32)
        - step_rate * block_scale[:, None, None] * precond_rows.astype(jnp.float32)
    ).astype(jnp.bfloat16)
    new_params = lax.all_gather(updated, "rep", axis=0, tiled=True)
    return (new_params, new_accum)


def solution(mesh):
    in_specs = (
        P("rep", None, "group", None),
        P("rep", "group", None),
        P("rep", "group", None),
        P("rep", "group", None, None, None),
        P("rep", "group", None, None, None),
        P(),
        P(),
    )
    out_specs = (P(None, "group", None), P("rep", "group", None))
    return jax.shard_map(local, mesh=mesh, in_specs=in_specs, out_specs=out_specs, check_vma=False)
```

profile of v0, /device:TPU:0, one launch (start us, length us, event | category | flops | bytes accessed | tf_op | source)
XLA Modules:
  0.0 279.0 jit_solution(11084299918333157456)
XLA Ops:
  7.2 0.0 copy-start
  7.2 0.0 reduce-scatter.2.cloned.1.call-start
  7.2 0.0 copy-start.1
  7.2 0.7 reduce-scatter.2.cloned.1.call-update
  7.9 0.1 copy-done.1
  8.1 64.1 %reduce-scatter.2.cloned.1.call-done = bf16[6,128,1024]{2,1,0:T(8,128)(2,1)} async-done(((bf16[24,128,1024]{2,1,0:T(8,128)(2,1)}), bf16[6,128,1024]{2,1,0:T(8,128)(2,1)}) %reduce-scatter.2.cloned.1.call-update) | async-done | bytes 1572880 | tf_op jit(solution)/shard_map/reduce_scatter | solution.py:29
  72.1 3.4 %gather_fusion = bf16[8,128,1024]{2,1,0:T(8,128)(2,1)} fusion(bf16[6,128,1024]{2,1,0:T(8,128)(2,1)} %reduce-scatter.2.cloned.1.call-done, s32[1024]{0:T(1024)S(1)} %pad_clamp_fusion.1), kind=kCustom, calls=%fused_computation | custom fusion | bytes 4194336 | tf_op jit(solution)/shard_map/jit(_take)/gather | solution.py:47
  75.5 1.9 fusion.7
  77.4 53.5 %all_to_all.8 = bf16[8,1,128,1024]{3,2,1,0:T(8,128)(2,1)} all-to-all(bf16[8,1,128,1024]{3,2,1,0:T(8,128)(2,1)S(1)} %fusion.7), channel_id=1, replica_groups=mesh['group'=8,'rep'=4] {'group'}, dimensions={0} | all-to-all | bytes 4194304 | tf_op jit(solution)/shard_map/all_to_all | solution.py:50
  130.9 0.0 copy-done
  130.9 8.8 %multiply_reduce_fusion = (f32[]{:T(128)}, bf16[1024,1024]{1,0:T(8,128)(2,1)}) fusion(bf16[1,1,1,1024,1024]{4,3,2,1,0:T(8,128)(2,1)S(1)} %copy-done, bf16[1024,1024]{1,0:T(8,128)(2,1)} %bitcast.39, bf16[1,1,1,1024,1024]{4,3,2,1,0:T(8,128)(2,1)} %param.10), kind=kOutput, calls=%fused_computation.2 | convolution fusion | flops 4300210176 | bytes 8388612 | tf_op jit(solution)/shard_map/sij,sjk->sik/dot_general | solution.py:56
  139.8 0.0 copy-start.2
  139.8 4.5 %all-to-all-start.1 = ((bf16[1,1,8,128,1024]{4,3,1,0,2:T(8,128)(2,1)}), bf16[1,1,8,128,1024]{4,3,1,0,2:T(8,128)(2,1)}, u32[]{:S(2)}, u32[]{:S(2)}) async-start(bf16[1,1,8,128,1024]{4,3,1,0,2:T(8,128)(2,1)} %bitcast.38), calls=%async_computation.2 | async-start | bytes 4194304 | tf_op jit(solution)/shard_map/all_to_all | solution.py:17
  144.2 0.0 all-gather.2.cloned.1.call-start
  144.3 0.6 constant_dynamic-slice_fusion.1
  144.9 0.0 copy-done.2
  144.9 0.1 dynamic_slice.11
  145.0 0.6 compare_convert_fusion
  145.6 0.1 select_reduce_fusion
  145.7 0.1 fusion.18
  145.9 4.7 %fusion.2 = (f32[6]{0:T(128)S(1)}, f32[6,128,1024]{2,1,0:T(8,128)}) fusion(bf16[6,128,1024]{2,1,0:T(8,128)(2,1)} %reduce-scatter.2.cloned.1.call-done, f32[6,128,1024]{2,1,0:T(8,128)} %param.9), kind=kLoop, calls=%fused_computation.7 | loop fusion | flops 4718586 | bytes 7864344 | tf_op jit(solution)/shard_map/reduce_sum | solution.py:38
  150.6 0.1 select_reduce_fusion.2
  150.7 0.6 broadcast_multiply_fusion.1
  151.3 59.8 %all-reduce = (f32[8]{0:T(128)S(1)}, f32[8]{0:T(128)S(1)}) all-reduce(f32[8]{0:T(128)S(1)} %broadcast_multiply_fusion.1, f32[8]{0:T(128)S(1)} %select_reduce_fusion.2), channel_id=1, replica_groups=mesh['group'=8,'rep'=4] {'group','rep'}, use_global_device_ids=true, to_apply=%region_6.7 | all-reduce | flops 16 | bytes 128 | tf_op jit(solution)/shard_map/psum | solution.py:76
  211.1 0.2 select_reduce_fusion.1
  211.2 0.0 all-to-all-done.1
  211.3 3.4 %gather_fusion.1 = bf16[6,128,1024]{2,1,0:T(8,128)(2,1)} fusion(bf16[8,128,1024]{2,1,0:T(8,128)(2,1)} %bitcast.10, s32[1024]{0:T(1024)S(1)} %pad_clamp_fusion), kind=kCustom, calls=%fused_computation.1 | custom fusion | bytes 3145752 | tf_op jit(solution)/shard_map/jit(_take)/gather | solution.py:78
  214.7 4.0 %subtract_convert_fusion = bf16[6,128,1024]{2,1,0:T(8,128)(2,1)} fusion(bf16[6,128,1024]{2,1,0:T(8,128)(2,1)} %param.8, bf16[6,128,1024]{2,1,0:T(8,128)(2,1)} %gather_fusion.1, f32[6]{0:T(128)S(1)} %broadcast_multiply_fusion, pred[6]{0:T(512)(128)(4,1)S(1)} %compare_and_fusion), kind=kLoop, calls=%fused_computation.8 | loop fusion | flops 4718592 | bytes 4718622 | tf_op jit(solution)/shard_map/convert_element_type | solution.py:84
  218.6 0.0 all-gather.2.cloned.1.call-update
  218.7 47.0 %all-gather.2.cloned.1.call-done = bf16[24,128,1024]{2,1,0:T(8,128)(2,1)} async-done(((bf16[6,128,1024]{2,1,0:T(8,128)(2,1)}), bf16[24,128,1024]{2,1,0:T(8,128)(2,1)}) %all-gather.2.cloned.1.call-update) | async-done | bytes 6291472 | tf_op jit(solution)/shard_map/all_gather | solution.py:85
  265.6 6.6 %copy.12 = bf16[24,128,1024]{2,1,0:T(8,128)(2,1)} copy(bf16[24,128,1024]{2,1,0:T(8,128)(2,1)} %all-gather.2.cloned.1.call-done) | data formatting | bytes 12582912
  (9 shorter events, 0.1 us)
Async XLA Ops:
  7.2 123.8 %copy-start = (bf16[1,1,1,1024,1024]{4,3,2,1,0:T(8,128)(2,1)S(1)}, bf16[1,1,1,1024,1024]{4,3,2,1,0:T(8,128)(2,1)}, u32[]{:S(2)}) copy-start(bf16[1,1,1,1024,1024]{4,3,2,1,0:T(8,128)(2,1)} %param.11) | copy-start | bytes 6291460
  7.2 65.0 %reduce-scatter.2.cloned.1.call-start = ((), (), s32[]{:S(2)}) async-start(), calls=%async_computation.3 | async-start | bytes 7864320 | tf_op jit(solution)/shard_map/reduce_scatter | solution.py:29
  7.2 0.8 copy-start.1
  139.8 5.1 %copy-start.2 = (s32[24]{0:T(128)S(1)}, s32[24]{0:T(128)}, u32[]{:S(2)}) copy-start(s32[24]{0:T(128)} %param.13) | copy-start | bytes 292
  139.8 71.5 %all-to-all-start.1 = ((bf16[1,1,8,128,1024]{4,3,1,0,2:T(8,128)(2,1)}), bf16[1,1,8,128,1024]{4,3,1,0,2:T(8,128)(2,1)}, u32[]{:S(2)}, u32[]{:S(2)}) async-start(bf16[1,1,8,128,1024]{4,3,1,0,2:T(8,128)(2,1)} %bitcast.38), calls=%async_computation.2 | async-start | bytes 4194304 | tf_op jit(solution)/shard_map/all_to_all | solution.py:17
  144.2 121.4 %all-gather.2.cloned.1.call-start = ((), (), s32[]{:S(2)}) async-start(), calls=%async_computation.4 | async-start | bytes 7864320 | tf_op jit(solution)/shard_map/all_gather | solution.py:85
Sparse Core Ops, SparseCore 0:
  10.5 61.5 reduce-scatter.1
  218.8 46.8 all-gather.1
where the time goes:
time: 280 us; the launch traced here: 279 us
  blocking collectives  113 us (40%)
  waiting for transfers between devices  112 us (40%)
  local copies, waits for them, and re-layouts  14.2 us (5%)
  between operations  14.2 us (5%)
  other arithmetic  12.3 us (4%)
  matrix products  8.83 us (3%)
  starting transfers between devices  4.55 us (2%)
    reduce_scatter x1, waiting for transfers between devices, local(): lax.psum_scatter(grad_parts[0].astype(jnp.float32).astype(jnp.bfloat16),...  64.1 us
    psum x1, blocking collectives, local(): lax.psum((graft_layer, shampoo_part), ('group', 'rep'))  59.8 us
    all_to_all x1, blocking collectives, local(): lax.all_to_all(outgoing, 'group', split_axis=0, concat_axis=2, tiled=True)  53.5 us
    all_gather x1, waiting for transfers between devices, local(): new_params = lax.all_gather(updated, 'rep', axis=0, tiled=True)  47 us
    dot_general x1, matrix products, local(): jnp.einsum('sij,sjk->sik', left_product, rights, preferred_element_type=j...  8.83 us
    unnamed x7, local copies, waits for them, and re-layouts  6.71 us
  transfers between devices with their start and end apart: 3, of which 2 were waited for; matrix products, arithmetic and copies ran while one was open for 3% of the time, Pallas kernels for 0%

commit v1 on v0

v1 whole, which is shorter than its diff:
```python
import functools

import jax
import jax.numpy as jnp
from jax import lax
from jax.experimental import pallas as pl
from jax.experimental.pallas import tpu as pltpu
from jax.sharding import PartitionSpec as P

MESH = pl.DeviceIdType.MESH
LAYERS = 8
LANES = 128
step_rate = 0.5
F32 = jnp.float32
BF16 = jnp.bfloat16


def kernel(
    n, chunks, width, rb, rows, size, tile,
    table, layer_of, grad, params, accum, left, right,
    new_params, new_accum,
    own, pair_in, half_out, half_in, summed, slot_out, block_in, lefts, rights, total, precond,
    rows_in, param_in, updated, other_in, acc, graft_sq, shampoo_sq, scales, stat_mine, stat_group, stat_rep,
    load_sem, pair_send, pair_recv, half_send, half_recv, slot_send, slot_recv, back_send, back_recv,
    stat_send, stat_recv, stat_rep_send, stat_rep_recv, other_send, other_recv, core_send, core_recv,
    store_sem,
):
    g = lax.axis_index("group")
    r = lax.axis_index("rep")
    pair = r + 1 - 2 * (r % 2)
    half = r + 2 - 4 * ((r // 2) % 2)
    pair_half = pair + 2 - 4 * ((pair // 2) % 2)

    def cols(c):
        return pl.ds(c * width, width)

    def blocks(q):
        return pl.ds(q * rb, rb)

    def peer(k):
        return (g + 1 + (n // 2 - 1 + k) % (n - 1)) % n

    def remote(src, dst, send, recv, where):
        return pltpu.make_async_remote_copy(
            src_ref=src, dst_ref=dst, send_sem=send, recv_sem=recv, device_id=where, device_id_type=MESH
        )

    def load_own(c, which):
        q = (r, half)[which]
        return pltpu.make_async_copy(grad.at[0, blocks(q), :, cols(c)], own.at[c, which], load_sem.at[which, c])

    def load_accum(c):
        return pltpu.make_async_copy(accum.at[:, :, cols(c)], acc.at[c], load_sem.at[2, c])

    def load_param(c):
        return pltpu.make_async_copy(params.at[:, :, cols(c)], param_in.at[c], load_sem.at[3, c])

    load_left = pltpu.make_async_copy(left.at[0, 0, 0], lefts, load_sem.at[4, 0])
    load_right = pltpu.make_async_copy(right.at[0, 0, 0], rights, load_sem.at[4, 1])

    def store_accum(c):
        return pltpu.make_async_copy(acc.at[c], new_accum.at[:, :, cols(c)], store_sem.at[0, c])

    def send_pair(c, which):
        q = (pair, pair_half)[which]
        return remote(
            grad.at[0, blocks(q), :, cols(c)], pair_in.at[c, which],
            pair_send.at[c, which], pair_recv.at[c, which], {"rep": pair},
        )

    def send_half(c):
        return remote(half_out.at[c], half_in.at[c], half_send.at[c], half_recv.at[c], {"rep": half})

    def send_slot(c, d):
        return remote(
            slot_out.at[c, d], block_in.at[c, pl.ds(g * rows, rows), :],
            slot_send.at[c, d], slot_recv.at[c, g], {"group": d},
        )

    def recv_slot(c, d):
        return remote(
            slot_out.at[c, d], block_in.at[c, pl.ds(d * rows, rows), :],
            slot_send.at[c, d], slot_recv.at[c, d], {"group": d},
        )

    def send_back(c, d):
        return remote(
            precond.at[c, pl.ds(d * rows, rows), :], rows_in[c].at[g],
            back_send.at[c, d], back_recv.at[c, g], {"group": d},
        )

    def recv_back(c, d):
        return remote(
            precond.at[c, pl.ds(d * rows, rows), :], rows_in[c].at[d],
            back_send.at[c, d], back_recv.at[c, d], {"group": d},
        )

    def send_stat(d):
        return remote(stat_mine, stat_group.at[g], stat_send.at[d], stat_recv.at[g], {"group": d})

    def recv_stat(d):
        return remote(stat_mine, stat_group.at[d], stat_send.at[d], stat_recv.at[d], {"group": d})

    def send_stat_rep(i, where):
        return remote(
            stat_rep.at[2 * i], stat_rep.at[2 * i + 1], stat_rep_send.at[i], stat_rep_recv.at[i], {"rep": where}
        )

    def send_other(c):
        return remote(updated.at[c], other_in.at[c], other_send.at[c], other_recv.at[c], {"rep": half})

    def send_core(c, which):
        src = (updated, other_in)[which]
        q = (r, half)[which]
        return remote(
            src.at[c], new_params.at[blocks(q), :, cols(c)],
            core_send.at[c, which], core_recv.at[c, which], {"rep": pair},
        )

    def recv_core(c, which):
        src = (updated, other_in)[which]
        q = (pair, pair_half)[which]
        return remote(
            src.at[c], new_params.at[blocks(q), :, cols(c)],
            core_send.at[c, which], core_recv.at[c, which], {"rep": pair},
        )

    def store_param(c, which):
        src = (updated, other_in)[which]
        q = (r, half)[which]
        return pltpu.make_async_copy(src.at[c], new_params.at[blocks(q), :, cols(c)], store_sem.at[1 + which, c])

    def each_peer(act):
        def body(k, carry):
            act(peer(k))
            return carry

        lax.fori_loop(0, n - 1, body, 0)

    for c in range(chunks):
        load_own(c, 1).start()
        load_own(c, 0).start()

    barrier = pltpu.get_barrier_semaphore()
    each_peer(
        lambda d: pl.semaphore_signal(barrier, inc=1, device_id={"group": d}, device_id_type=MESH)
    )
    pl.semaphore_signal(barrier, inc=1, device_id={"rep": pair}, device_id_type=MESH)
    pl.semaphore_signal(barrier, inc=1, device_id={"rep": half}, device_id_type=MESH)
    pl.semaphore_wait(barrier, n + 1)

    for c in range(chunks):
        send_pair(c, 1).start()
        send_pair(c, 0).start()
    for c in range(chunks):
        load_accum(c).start()
    load_left.start()
    load_right.start()
    for c in range(chunks):
        load_param(c).start()

    graft_sq[...] = jnp.zeros_like(graft_sq)
    shampoo_sq[...] = jnp.zeros_like(shampoo_sq)

    for c in range(chunks):
        load_own(c, 1).wait()
        send_pair(c, 1).wait_recv()

        def add_pair(j, carry):
            half_out[c, j] = (own[c, 1, j].astype(F32) + pair_in[c, 1, j].astype(F32)).astype(BF16)
            return carry

        lax.fori_loop(0, rb, add_pair, 0)
        send_half(c).start()

    def sum_and_send(c):
        load_own(c, 0).wait()
        send_pair(c, 0).wait_recv()
        send_half(c).wait_recv()

        def add_half(j, carry):
            summed[c, j] = (
                own[c, 0, j].astype(F32) + pair_in[c, 0, j].astype(F32) + half_in[c, j].astype(F32)
            ).astype(BF16)
            return carry

        lax.fori_loop(0, rb, add_half, 0)

        def fill(d, carry):
            slot_out[c, d] = summed[c, jnp.maximum(table[r, d, 0], 0)]
            return carry

        lax.fori_loop(0, n, fill, 0)
        each_peer(lambda d: send_slot(c, d).start())
        block_in[c, pl.ds(g * rows, rows), :] = slot_out[c, g]

        load_accum(c).wait()

        def graft(j, carry):
            gradient = summed[c, j].astype(F32)
            now = acc[c, j] + gradient * gradient
            acc[c, j] = now
            scaled = gradient * lax.rsqrt(now)
            graft_sq[j] += jnp.sum((scaled * scaled).reshape(rows // 8, 8, width), axis=0)
            return carry

        lax.fori_loop(0, rb, graft, 0)
        store_accum(c).start()

    def multiply(c):
        each_peer(lambda d: recv_slot(c, d).wait_recv())
        if c == 0:
            load_left.wait()
            load_right.wait()

        def body(i, carry):
            at = pl.ds(pl.multiple_of(i * tile, tile), tile)
            product = jnp.dot(lefts[at, :], block_in[c], preferred_element_type=F32).astype(BF16)
            part = jnp.dot(product, rights[c * width : (c + 1) * width, :], preferred_element_type=F32)
            if c > 0:
                part = total[at, :] + part
            if c < chunks - 1:
                total[at, :] = part
            else:
                out = part.astype(BF16)
                wide = out.astype(F32)
                shampoo_sq[...] += jnp.sum((wide * wide).reshape(tile // 8, 8, size), axis=0)
                for e in range(chunks):
                    precond[e, at, :] = out[:, e * width : (e + 1) * width]
            return carry

        lax.fori_loop(0, size // tile, body, 0)

    for c in range(chunks + 2):
        if c >= 2:
            multiply(c - 2)
        if c < chunks:
            sum_and_send(c)

    lane = lax.broadcasted_iota(jnp.int32, (1, LANES), 1)
    mine = table[r, g, 0]
    mine_at = layer_of[r * rb + jnp.maximum(mine, 0)]
    used = jnp.where(mine >= 0, 1.0, 0.0).astype(F32)
    shampoo = jnp.where(lane == mine_at, used * jnp.sum(shampoo_sq[...], keepdims=True), 0.0)

    def layer_sum(j, carry):
        return carry + jnp.where(lane == layer_of[r * rb + j], jnp.sum(graft_sq[j], keepdims=True), 0.0)

    graft_total = lax.fori_loop(0, rb, layer_sum, jnp.zeros((1, LANES), F32))
    row = lax.broadcasted_iota(jnp.int32, (8, LANES), 0)
    stat = jnp.where(row == 0, graft_total, 0.0) + jnp.where(row == 1, shampoo, 0.0)
    stat_mine[...] = stat
    stat_group[g] = stat
    each_peer(lambda d: send_stat(d).start())
    for c in range(chunks):
        each_peer(lambda d: send_back(c, d).start())
    for c in range(chunks):
        rows_in[c][g] = precond[c, pl.ds(pl.multiple_of(g * rows, rows), rows), :]
    each_peer(lambda d: recv_stat(d).wait_recv())
    stat_rep[0] = jnp.sum(stat_group[...], axis=0)
    send_stat_rep(0, pair).start()
    send_stat_rep(0, pair).wait_recv()
    stat_rep[2] = stat_rep[0] + stat_rep[1]
    send_stat_rep(1, half).start()
    send_stat_rep(1, half).wait_recv()
    stat = stat_rep[2] + stat_rep[3]
    layer_scale = jnp.sqrt(stat[0:1]) * lax.rsqrt(stat[1:2] + 1e-06)

    def block_scale(j, carry):
        scale = jnp.sum(jnp.where(lane == layer_of[r * rb + j], layer_scale, 0.0), axis=1, keepdims=True)
        scales[j] = jnp.broadcast_to(step_rate * scale, (1, width))
        return carry

    lax.fori_loop(0, rb, block_scale, 0)

    def pass_on(c):
        send_other(c).wait_recv()
        send_core(c, 1).start()
        store_param(c, 1).start()

    for c in range(chunks):
        load_param(c).wait()
        each_peer(lambda d: recv_back(c, d).wait_recv())

        def update(j, carry):
            def find(d, at):
                return jnp.where(table[r, d, 0] == j, d, at)

            position = lax.fori_loop(0, n, find, 0)
            updated[c, j] = (param_in[c, j].astype(F32) - scales[j] * rows_in[c][position].astype(F32)).astype(BF16)
            return carry

        lax.fori_loop(0, rb, update, 0)
        send_other(c).start()
        send_core(c, 0).start()
        store_param(c, 0).start()
        if c > 0:
            pass_on(c - 1)
    pass_on(chunks - 1)

    for c in range(chunks):
        store_accum(c).wait()
        for which in range(2):
            store_param(c, which).wait()
            send_core(c, which).wait_send()
            recv_core(c, which).wait_recv()
            send_pair(c, which).wait_send()
        send_half(c).wait_send()
        send_other(c).wait_send()
        each_peer(lambda d: send_slot(c, d).wait_send())
        each_peer(lambda d: send_back(c, d).wait_send())
    each_peer(lambda d: send_stat(d).wait_send())
    send_stat_rep(0, pair).wait_send()
    send_stat_rep(1, half).wait_send()


CHUNKS = 4


def local(grad_parts, params, accum, left_pre, right_pre, slot_block, layer_of):
    n = lax.axis_size("group")
    assert lax.axis_size("rep") == 4 and left_pre.shape[2] == 1
    rb, rows, size = params.shape
    chunks = CHUNKS
    width = size // chunks
    tile = 256
    any_space = pl.BlockSpec(memory_space=pl.ANY)
    scalars = pl.BlockSpec(memory_space=pltpu.SMEM)
    dma = pltpu.SemaphoreType.DMA
    part = (chunks, rb, rows, width)
    twice = (chunks, 2, rb, rows, width)
    slots = (chunks, n, rows, width)
    whole = (chunks, size, width)
    vmem = pltpu.VMEM
    return pl.pallas_call(
        functools.partial(kernel, n, chunks, width, rb, rows, size, tile),
        out_shape=(
            jax.ShapeDtypeStruct((grad_parts.shape[1], rows, size), BF16),
            jax.ShapeDtypeStruct(accum.shape, F32),
        ),
        in_specs=[scalars] * 2 + [any_space] * 5,
        out_specs=(any_space, any_space),
        scratch_shapes=[
            vmem(twice, BF16), vmem(twice, BF16), vmem(part, BF16), vmem(part, BF16), vmem(part, BF16),
            vmem(slots, BF16), vmem(whole, BF16), vmem((size, size), BF16), vmem((size, size), BF16),
            vmem((size, size), F32), vmem(whole, BF16),
            [vmem(slots[1:], BF16)] * chunks, vmem(part, BF16), vmem(part, BF16), vmem(part, BF16), vmem(part, F32),
            vmem((rb, 8, width), F32), vmem((8, size), F32), vmem((rb, 1, width), F32),
            vmem((8, LANES), F32), vmem((n, 8, LANES), F32), vmem((4, 8, LANES), F32),
            dma((5, max(chunks, 2))), dma((chunks, 2)), dma((chunks, 2)), dma((chunks,)), dma((chunks,)),
            dma((chunks, n)), dma((chunks, n)), dma((chunks, n)), dma((chunks, n)),
            dma((n,)), dma((n,)), dma((2,)), dma((2,)), dma((chunks,)), dma((chunks,)),
            dma((chunks, 2)), dma((chunks, 2)), dma((3, chunks)),
        ],
        compiler_params=pltpu.CompilerParams(
            collective_id=0, has_side_effects=True, vmem_limit_bytes=60 * 1024 * 1024
        ),
    )(slot_block, layer_of, grad_parts, params, accum, left_pre, right_pre)


def solution(mesh):
    in_specs = (
        P("rep", None, "group", None),
        P("rep", "group", None),
        P("rep", "group", None),
        P("rep", "group", None, None, None),
        P("rep", "group", None, None, None),
        P(),
        P(),
    )
    out_specs = (P(None, "group", None), P("rep", "group", None))
    return jax.shard_map(local, mesh=mesh, in_specs=in_specs, out_specs=out_specs, check_vma=False)
```

time: 280 us -> 149 us (0.53)
  Pallas kernels: 0 us -> 138 us
  blocking collectives: 113 us -> 0 us
  waiting for transfers between devices: 112 us -> 0 us
  between operations: 14.2 us -> 0.65 us
  other arithmetic: 12.3 us -> 0 us
  matrix products: 8.83 us -> 0 us
  starting transfers between devices: 4.55 us -> 0 us
  local copies, waits for them, and re-layouts: 14.2 us -> 9.76 us
    pallas_call x0 -> x1, Pallas kernels: none -> 138 us  [local(): pl.pallas_call(functools.partial(kernel, n, chunks, width, rb, rows, size...]
    reduce_scatter x1 -> x0, waiting for transfers between devices: 64.1 us -> none  [local(): lax.psum_scatter(grad_parts[0].astype(jnp.float32).astype(jnp.bfloat16),...]
    psum x1 -> x0, blocking collectives: 59.8 us -> none  [local(): lax.psum((graft_layer, shampoo_part), ('group', 'rep'))]
    all_to_all x1 -> x0, blocking collectives: 53.5 us -> none  [local(): lax.all_to_all(outgoing, 'group', split_axis=0, concat_axis=2, tiled=True)]
    all_gather x1 -> x0, waiting for transfers between devices: 47 us -> none  [local(): new_params = lax.all_gather(updated, 'rep', axis=0, tiled=True)]
    dot_general x1 -> x0, matrix products: 8.83 us -> none  [local(): jnp.einsum('sij,sjk->sik', left_product, rights, preferred_element_type=j...]
    gather x2 -> x0, local copies, waits for them, and re-layouts: 6.84 us -> none  [the longest x1 3.43 us: local(): precond_rows = jnp.take(returned, position, axis=0)]
    reduce_sum x5 -> x0, other arithmetic: 5.23 us -> none  [the longest x1 4.74 us: local(): graft_blocks = jnp.sum(graft * graft, axis=(1, 2))]
  transfers between devices with their start and end apart: 3 -> 0, of which waited for: 2 -> 0; matrix products, arithmetic and copies ran while one was open for 3% -> 0% of each run, Pallas kernels for 0% -> 0%
where the time goes in v1:
time: 149 us; the launch traced here: 148 us
  Pallas kernels  138 us (93%)
  local copies, waits for them, and re-layouts  9.76 us (7%)
    pallas_call x1, Pallas kernels, local(): pl.pallas_call(functools.partial(kernel, n, chunks, width, rb, rows, size...  138 us
    unnamed x5, local copies, waits for them, and re-layouts  9.76 us

profile of v1, /device:TPU:0, one launch (start us, length us, event | category | flops | bytes accessed | tf_op | source)
XLA Modules:
  0.0 148.3 jit_solution(2614349795326710997)
XLA Ops:
  0.6 1.4 copy.9.table
  2.0 137.9 %shard_map.86 = (bf16[24,128,1024]{2,1,0:T(8,128)(2,1)}, f32[6,128,1024]{2,1,0:T(8,128)}) custom-call(s32[4,8,1]{2,1,0:T(8,128)} %copy.9.table, s32[24]{0:T(128)} %layer_of.1, bf16[1,24,128,1024]{3,2,1,0:T(8,128)(2,1)} %grad.1, bf16[6,128,1024]{2,1,0:T(8,128)(2,1)} %params.1, f32[6,128,1024]{2,1,0:T(8,128)} %accum.1, bf16[1,1,1,1024,1024]{4,3,2,1,0:T(8,128)(2,1)} %left.1, ...), custom_call_target="tpu_custom_call" | custom-call | tf_op jit(solution)/shard_map/pallas_call | solution.py:335
  139.9 0.0 copy-start
  139.9 6.7 %copy.12 = bf16[24,128,1024]{2,1,0:T(8,128)(2,1)} copy(bf16[24,128,1024]{2,1,0:T(8,128)(2,1)} %get-tuple-element.4) | data formatting | bytes 12582912
  146.7 0.0 copy-done
  146.7 1.7 %copy.13 = f32[6,128,1024]{2,1,0:T(8,128)} copy(f32[6,128,1024]{2,1,0:T(8,128)S(1)} %copy-done) | data formatting | bytes 6291456
Async XLA Ops:
  139.9 6.7 %copy-start = (f32[6,128,1024]{2,1,0:T(8,128)S(1)}, f32[6,128,1024]{2,1,0:T(8,128)}, u32[]{:S(2)}) copy-start(f32[6,128,1024]{2,1,0:T(8,128)} %get-tuple-element.5) | copy-start | bytes 9437188

commit v2 on v1

--- a/solution.py
+++ b/solution.py
@@ -17,13 +17,13 @@
 
 def kernel(
     n, chunks, width, rb, rows, size, tile,
-    table, layer_of, grad, params, accum, left, right,
+    table_in, layer_in, grad, params, accum, left, right,
     new_params, new_accum,
     own, pair_in, half_out, half_in, summed, slot_out, block_in, lefts, rights, total, precond,
     rows_in, param_in, updated, other_in, acc, graft_sq, shampoo_sq, scales, stat_mine, stat_group, stat_rep,
     load_sem, pair_send, pair_recv, half_send, half_recv, slot_send, slot_recv, back_send, back_recv,
     stat_send, stat_recv, stat_rep_send, stat_rep_recv, other_send, other_recv, core_send, core_recv,
-    store_sem,
+    store_sem, table, layer_of,
 ):
     g = lax.axis_index("group")
     r = lax.axis_index("rep")
@@ -55,6 +55,8 @@
     def load_param(c):
         return pltpu.make_async_copy(params.at[:, :, cols(c)], param_in.at[c], load_sem.at[3, c])
 
+    load_table = pltpu.make_async_copy(table_in, table, load_sem.at[0, chunks])
+    load_layers = pltpu.make_async_copy(layer_in, layer_of, load_sem.at[1, chunks])
     load_left = pltpu.make_async_copy(left.at[0, 0, 0], lefts, load_sem.at[4, 0])
     load_right = pltpu.make_async_copy(right.at[0, 0, 0], rights, load_sem.at[4, 1])
 
@@ -141,6 +143,8 @@
         load_own(c, 1).start()
         load_own(c, 0).start()
 
+    load_table.start()
+    load_layers.start()
     barrier = pltpu.get_barrier_semaphore()
     each_peer(
         lambda d: pl.semaphore_signal(barrier, inc=1, device_id={"group": d}, device_id_type=MESH)
@@ -159,6 +163,8 @@
     for c in range(chunks):
         load_param(c).start()
 
+    load_table.wait()
+    load_layers.wait()
     graft_sq[...] = jnp.zeros_like(graft_sq)
     shampoo_sq[...] = jnp.zeros_like(shampoo_sq)
 
@@ -187,7 +193,7 @@
         lax.fori_loop(0, rb, add_half, 0)
 
         def fill(d, carry):
-            slot_out[c, d] = summed[c, jnp.maximum(table[r, d, 0], 0)]
+            slot_out[c, d] = summed[c, jnp.maximum(table[r, 0, d], 0)]
             return carry
 
         lax.fori_loop(0, n, fill, 0)
@@ -238,7 +244,7 @@
             sum_and_send(c)
 
     lane = lax.broadcasted_iota(jnp.int32, (1, LANES), 1)
-    mine = table[r, g, 0]
+    mine = table[r, 0, g]
     mine_at = layer_of[r * rb + jnp.maximum(mine, 0)]
     used = jnp.where(mine >= 0, 1.0, 0.0).astype(F32)
     shampoo = jnp.where(lane == mine_at, used * jnp.sum(shampoo_sq[...], keepdims=True), 0.0)
@@ -284,7 +290,7 @@
 
         def update(j, carry):
             def find(d, at):
-                return jnp.where(table[r, d, 0] == j, d, at)
+                return jnp.where(table[r, 0, d] == j, d, at)
 
             position = lax.fori_loop(0, n, find, 0)
             updated[c, j] = (param_in[c, j].astype(F32) - scales[j] * rows_in[c][position].astype(F32)).astype(BF16)
@@ -314,7 +320,7 @@
     send_stat_rep(1, half).wait_send()
 
 
-CHUNKS = 4
+CHUNKS = 8
 
 
 def local(grad_parts, params, accum, left_pre, right_pre, slot_block, layer_of):
@@ -325,20 +331,21 @@
     width = size // chunks
     tile = 256
     any_space = pl.BlockSpec(memory_space=pl.ANY)
-    scalars = pl.BlockSpec(memory_space=pltpu.SMEM)
     dma = pltpu.SemaphoreType.DMA
     part = (chunks, rb, rows, width)
     twice = (chunks, 2, rb, rows, width)
     slots = (chunks, n, rows, width)
     whole = (chunks, size, width)
     vmem = pltpu.VMEM
+    operands = (jnp.swapaxes(slot_block, 1, 2), layer_of, grad_parts, params, accum, left_pre, right_pre)
+    operands = [pltpu.with_memory_space_constraint(x, pltpu.HBM) for x in operands]
     return pl.pallas_call(
         functools.partial(kernel, n, chunks, width, rb, rows, size, tile),
         out_shape=(
             jax.ShapeDtypeStruct((grad_parts.shape[1], rows, size), BF16),
             jax.ShapeDtypeStruct(accum.shape, F32),
         ),
-        in_specs=[scalars] * 2 + [any_space] * 5,
+        in_specs=[pl.BlockSpec(memory_space=pltpu.HBM)] * 7,
         out_specs=(any_space, any_space),
         scratch_shapes=[
             vmem(twice, BF16), vmem(twice, BF16), vmem(part, BF16), vmem(part, BF16), vmem(part, BF16),
@@ -347,15 +354,16 @@
             [vmem(slots[1:], BF16)] * chunks, vmem(part, BF16), vmem(part, BF16), vmem(part, BF16), vmem(part, F32),
             vmem((rb, 8, width), F32), vmem((8, size), F32), vmem((rb, 1, width), F32),
             vmem((8, LANES), F32), vmem((n, 8, LANES), F32), vmem((4, 8, LANES), F32),
-            dma((5, max(chunks, 2))), dma((chunks, 2)), dma((chunks, 2)), dma((chunks,)), dma((chunks,)),
+            dma((5, chunks + 1)), dma((chunks, 2)), dma((chunks, 2)), dma((chunks,)), dma((chunks,)),
             dma((chunks, n)), dma((chunks, n)), dma((chunks, n)), dma((chunks, n)),
             dma((n,)), dma((n,)), dma((2,)), dma((2,)), dma((chunks,)), dma((chunks,)),
             dma((chunks, 2)), dma((chunks, 2)), dma((3, chunks)),
+            pltpu.SMEM((slot_block.shape[0], 1, n), jnp.int32), pltpu.SMEM(layer_of.shape, jnp.int32),
         ],
         compiler_params=pltpu.CompilerParams(
-            collective_id=0, has_side_effects=True, vmem_limit_bytes=60 * 1024 * 1024
+            collective_id=0, has_side_effects=True, vmem_limit_bytes=38 * 1024 * 1024
         ),
-    )(slot_block, layer_of, grad_parts, params, accum, left_pre, right_pre)
+    )(*operands)
 
 
 def solution(mesh):

time: 149 us -> 134 us (0.90)
  Pallas kernels: 138 us -> 129 us
  local copies, waits for them, and re-layouts: 9.76 us -> 4.37 us
    pallas_call x1, Pallas kernels: 138 us -> 129 us  [local(): pl.pallas_call(functools.partial(kernel, n, chunks, width, rb, rows, size...]
    unnamed x5 -> x2, local copies, waits for them, and re-layouts: 9.76 us -> 4.37 us
where the time goes in v2:
time: 134 us
  Pallas kernels  129 us (96%)
  local copies, waits for them, and re-layouts  4.37 us (3%)
    pallas_call x1, Pallas kernels, local(): pl.pallas_call(functools.partial(kernel, n, chunks, width, rb, rows, size...  129 us
    unnamed x2, local copies, waits for them, and re-layouts  4.37 us

profile of v2, /device:TPU:0, one launch (start us, length us, event | category | flops | bytes accessed | tf_op | source)
XLA Modules:
  0.0 134.0 jit_solution(11783952874113386313)
XLA Ops:
  0.6 129.0 %shard_map.86 = (bf16[24,128,1024]{2,1,0:T(8,128)(2,1)S(1)}, f32[6,128,1024]{2,1,0:T(8,128)S(1)}) custom-call(s32[4,1,8]{2,1,0:T(1,128)} %bitcast.3, s32[24]{0:T(128)} %layer_in.1, bf16[1,24,128,1024]{3,2,1,0:T(8,128)(2,1)} %grad.1, bf16[6,128,1024]{2,1,0:T(8,128)(2,1)} %params.1, f32[6,128,1024]{2,1,0:T(8,128)} %accum.1, ...), custom_call_target="tpu_custom_call" | custom-call | tf_op jit(solution)/shard_map/pallas_call | solution.py:342
  129.6 2.7 %copy.12 = bf16[24,128,1024]{2,1,0:T(8,128)(2,1)} copy(bf16[24,128,1024]{2,1,0:T(8,128)(2,1)S(1)} %get-tuple-element.4) | data formatting | bytes 12582912
  132.3 1.7 %copy.13 = f32[6,128,1024]{2,1,0:T(8,128)} copy(f32[6,128,1024]{2,1,0:T(8,128)S(1)} %get-tuple-element.5) | data formatting | bytes 6291456

commit v3 on v2

--- a/solution.py
+++ b/solution.py
@@ -31,6 +31,12 @@
     half = r + 2 - 4 * ((r // 2) % 2)
     pair_half = pair + 2 - 4 * ((pair // 2) % 2)
 
+    part = rows // 2
+    ahead = ((0, 0, part), (0, part, part)) + tuple((c, 0, rows) for c in range(1, chunks))
+    final = chunks - 1
+    behind = tuple((c, 0, rows) for c in range(final)) + ((final, 0, part), (final, part, part))
+    pieces = chunks + 1
+
     def cols(c):
         return pl.ds(c * width, width)
 
@@ -70,32 +76,38 @@
             pair_send.at[c, which], pair_recv.at[c, which], {"rep": pair},
         )
 
-    def send_half(c):
-        return remote(half_out.at[c], half_in.at[c], half_send.at[c], half_recv.at[c], {"rep": half})
-
-    def send_slot(c, d):
-        return remote(
-            slot_out.at[c, d], block_in.at[c, pl.ds(g * rows, rows), :],
-            slot_send.at[c, d], slot_recv.at[c, g], {"group": d},
-        )
-
-    def recv_slot(c, d):
-        return remote(
-            slot_out.at[c, d], block_in.at[c, pl.ds(d * rows, rows), :],
-            slot_send.at[c, d], slot_recv.at[c, d], {"group": d},
-        )
-
-    def send_back(c, d):
-        return remote(
-            precond.at[c, pl.ds(d * rows, rows), :], rows_in[c].at[g],
-            back_send.at[c, d], back_recv.at[c, g], {"group": d},
-        )
-
-    def recv_back(c, d):
-        return remote(
-            precond.at[c, pl.ds(d * rows, rows), :], rows_in[c].at[d],
-            back_send.at[c, d], back_recv.at[c, d], {"group": d},
-        )
+    def send_half(p):
+        c, a, m = ahead[p]
+        return remote(
+            half_out.at[c, :, pl.ds(a, m), :], half_in.at[c, :, pl.ds(a, m), :],
+            half_send.at[p], half_recv.at[p], {"rep": half},
+        )
+
+    def slot(p, d, source):
+        c, a, m = ahead[p]
+        return remote(
+            slot_out.at[c, d, pl.ds(a, m), :], block_in.at[c, pl.ds(source * rows + a, m), :],
+            slot_send.at[p, d], slot_recv.at[p, source], {"group": d},
+        )
+
+    def send_slot(p, d):
+        return slot(p, d, g)
+
+    def recv_slot(p, d):
+        return slot(p, d, d)
+
+    def back(p, d, source):
+        c, a, m = behind[p]
+        return remote(
+            precond.at[c, pl.ds(d * rows + a, m), :], rows_in[p].at[source],
+            back_send.at[p, d], back_recv.at[p, source], {"group": d},
+        )
+
+    def send_back(p, d):
+        return back(p, d, g)
+
+    def recv_back(p, d):
+        return back(p, d, d)
 
     def send_stat(d):
         return remote(stat_mine, stat_group.at[g], stat_send.at[d], stat_recv.at[g], {"group": d})
@@ -108,29 +120,29 @@
             stat_rep.at[2 * i], stat_rep.at[2 * i + 1], stat_rep_send.at[i], stat_rep_recv.at[i], {"rep": where}
         )
 
-    def send_other(c):
-        return remote(updated.at[c], other_in.at[c], other_send.at[c], other_recv.at[c], {"rep": half})
-
-    def send_core(c, which):
+    def send_other(p):
+        c, a, m = behind[p]
+        return remote(
+            updated.at[c, :, pl.ds(a, m), :], other_in.at[c, :, pl.ds(a, m), :],
+            other_send.at[p], other_recv.at[p], {"rep": half},
+        )
+
+    def result(p, which, q):
+        c, a, m = behind[p]
         src = (updated, other_in)[which]
-        q = (r, half)[which]
-        return remote(
-            src.at[c], new_params.at[blocks(q), :, cols(c)],
-            core_send.at[c, which], core_recv.at[c, which], {"rep": pair},
-        )
-
-    def recv_core(c, which):
-        src = (updated, other_in)[which]
-        q = (pair, pair_half)[which]
-        return remote(
-            src.at[c], new_params.at[blocks(q), :, cols(c)],
-            core_send.at[c, which], core_recv.at[c, which], {"rep": pair},
-        )
-
-    def store_param(c, which):
-        src = (updated, other_in)[which]
-        q = (r, half)[which]
-        return pltpu.make_async_copy(src.at[c], new_params.at[blocks(q), :, cols(c)], store_sem.at[1 + which, c])
+        return src.at[c, :, pl.ds(a, m), :], new_params.at[blocks(q), pl.ds(a, m), cols(c)]
+
+    def send_core(p, which):
+        src, dst = result(p, which, (r, half)[which])
+        return remote(src, dst, core_send.at[p, which], core_recv.at[p, which], {"rep": pair})
+
+    def recv_core(p, which):
+        src, dst = result(p, which, (pair, pair_half)[which])
+        return remote(src, dst, core_send.at[p, which], core_recv.at[p, which], {"rep": pair})
+
+    def store_param(p, which):
+        src, dst = result(p, which, (r, half)[which])
+        return pltpu.make_async_copy(src, dst, store_sem.at[1 + which, p])
 
     def each_peer(act):
         def body(k, carry):
@@ -177,49 +189,62 @@
             return carry
 
         lax.fori_loop(0, rb, add_pair, 0)
-        send_half(c).start()
-
-    def sum_and_send(c):
-        load_own(c, 0).wait()
-        send_pair(c, 0).wait_recv()
-        send_half(c).wait_recv()
+        for p in range(pieces):
+            if ahead[p][0] == c:
+                send_half(p).start()
+
+    def sum_and_send(p):
+        c, a, m = ahead[p]
+        at = pl.ds(a, m)
+        if a == 0:
+            load_own(c, 0).wait()
+            send_pair(c, 0).wait_recv()
+        send_half(p).wait_recv()
 
         def add_half(j, carry):
-            summed[c, j] = (
-                own[c, 0, j].astype(F32) + pair_in[c, 0, j].astype(F32) + half_in[c, j].astype(F32)
+            summed[c, j, at, :] = (
+                own[c, 0, j, at, :].astype(F32) + pair_in[c, 0, j, at, :].astype(F32) + half_in[c, j, at, :].astype(F32)
             ).astype(BF16)
             return carry
 
         lax.fori_loop(0, rb, add_half, 0)
 
         def fill(d, carry):
-            slot_out[c, d] = summed[c, jnp.maximum(table[r, 0, d], 0)]
+            slot_out[c, d, at, :] = summed[c, jnp.maximum(table[r, 0, d], 0), at, :]
             return carry
 
         lax.fori_loop(0, n, fill, 0)
-        each_peer(lambda d: send_slot(c, d).start())
-        block_in[c, pl.ds(g * rows, rows), :] = slot_out[c, g]
-
-        load_accum(c).wait()
+        each_peer(lambda d: send_slot(p, d).start())
+        block_in[c, pl.ds(pl.multiple_of(g * rows + a, m), m), :] = slot_out[c, g, at, :]
+
+        if a == 0:
+            load_accum(c).wait()
 
         def graft(j, carry):
-            gradient = summed[c, j].astype(F32)
-            now = acc[c, j] + gradient * gradient
-            acc[c, j] = now
+            gradient = summed[c, j, at, :].astype(F32)
+            now = acc[c, j, at, :] + gradient * gradient
+            acc[c, j, at, :] = now
             scaled = gradient * lax.rsqrt(now)
-            graft_sq[j] += jnp.sum((scaled * scaled).reshape(rows // 8, 8, width), axis=0)
+            graft_sq[j] += jnp.sum((scaled * scaled).reshape(m // 8, 8, width), axis=0)
             return carry
 
         lax.fori_loop(0, rb, graft, 0)
-        store_accum(c).start()
+        if a + m == rows:
+            store_accum(c).start()
 
     def multiply(c):
-        each_peer(lambda d: recv_slot(c, d).wait_recv())
+        for p in range(pieces):
+            if ahead[p][0] == c:
+                each_peer(lambda d: recv_slot(p, d).wait_recv())
         if c == 0:
             load_left.wait()
             load_right.wait()
 
-        def body(i, carry):
+        tiles = size // tile
+        first = (g * rows) // tile + tiles // 2
+
+        def body(step, carry):
+            i = (first + step) % tiles
             at = pl.ds(pl.multiple_of(i * tile, tile), tile)
             product = jnp.dot(lefts[at, :], block_in[c], preferred_element_type=F32).astype(BF16)
             part = jnp.dot(product, rights[c * width : (c + 1) * width, :], preferred_element_type=F32)
@@ -233,15 +258,26 @@
                 shampoo_sq[...] += jnp.sum((wide * wide).reshape(tile // 8, 8, size), axis=0)
                 for e in range(chunks):
                     precond[e, at, :] = out[:, e * width : (e + 1) * width]
-            return carry
-
-        lax.fori_loop(0, size // tile, body, 0)
-
-    for c in range(chunks + 2):
-        if c >= 2:
-            multiply(c - 2)
-        if c < chunks:
-            sum_and_send(c)
+
+                def send_tile(k, carry):
+                    d = i * (tile // rows) + k
+
+                    @pl.when(d != g)
+                    def _():
+                        send_back(0, d).start()
+
+                    return carry
+
+                lax.fori_loop(0, tile // rows, send_tile, 0)
+            return carry
+
+        lax.fori_loop(0, tiles, body, 0)
+
+    for p in range(chunks + LAG):
+        if p >= LAG:
+            multiply(p - LAG)
+        if p < pieces:
+            sum_and_send(p)
 
     lane = lax.broadcasted_iota(jnp.int32, (1, LANES), 1)
     mine = table[r, 0, g]
@@ -258,10 +294,11 @@
     stat_mine[...] = stat
     stat_group[g] = stat
     each_peer(lambda d: send_stat(d).start())
-    for c in range(chunks):
-        each_peer(lambda d: send_back(c, d).start())
-    for c in range(chunks):
-        rows_in[c][g] = precond[c, pl.ds(pl.multiple_of(g * rows, rows), rows), :]
+    for p in range(1, pieces):
+        each_peer(lambda d: send_back(p, d).start())
+    for p in range(pieces):
+        c, a, m = behind[p]
+        rows_in[p][g] = precond[c, pl.ds(pl.multiple_of(g * rows + a, m), m), :]
     each_peer(lambda d: recv_stat(d).wait_recv())
     stat_rep[0] = jnp.sum(stat_group[...], axis=0)
     send_stat_rep(0, pair).start()
@@ -279,48 +316,56 @@
 
     lax.fori_loop(0, rb, block_scale, 0)
 
-    def pass_on(c):
-        send_other(c).wait_recv()
-        send_core(c, 1).start()
-        store_param(c, 1).start()
-
-    for c in range(chunks):
-        load_param(c).wait()
-        each_peer(lambda d: recv_back(c, d).wait_recv())
+    def pass_on(p):
+        send_other(p).wait_recv()
+        send_core(p, 1).start()
+        store_param(p, 1).start()
+
+    for p in range(pieces):
+        c, a, m = behind[p]
+        at = pl.ds(a, m)
+        if a == 0:
+            load_param(c).wait()
+        each_peer(lambda d: recv_back(p, d).wait_recv())
 
         def update(j, carry):
-            def find(d, at):
-                return jnp.where(table[r, 0, d] == j, d, at)
+            def find(d, found):
+                return jnp.where(table[r, 0, d] == j, d, found)
 
             position = lax.fori_loop(0, n, find, 0)
-            updated[c, j] = (param_in[c, j].astype(F32) - scales[j] * rows_in[c][position].astype(F32)).astype(BF16)
+            updated[c, j, at, :] = (
+                param_in[c, j, at, :].astype(F32) - scales[j] * rows_in[p][position].astype(F32)
+            ).astype(BF16)
             return carry
 
         lax.fori_loop(0, rb, update, 0)
-        send_other(c).start()
-        send_core(c, 0).start()
-        store_param(c, 0).start()
-        if c > 0:
-            pass_on(c - 1)
-    pass_on(chunks - 1)
+        send_other(p).start()
+        send_core(p, 0).start()
+        store_param(p, 0).start()
+        if p > 0:
+            pass_on(p - 1)
+    pass_on(pieces - 1)
 
     for c in range(chunks):
         store_accum(c).wait()
         for which in range(2):
-            store_param(c, which).wait()
-            send_core(c, which).wait_send()
-            recv_core(c, which).wait_recv()
             send_pair(c, which).wait_send()
-        send_half(c).wait_send()
-        send_other(c).wait_send()
-        each_peer(lambda d: send_slot(c, d).wait_send())
-        each_peer(lambda d: send_back(c, d).wait_send())
+    for p in range(pieces):
+        for which in range(2):
+            store_param(p, which).wait()
+            send_core(p, which).wait_send()
+            recv_core(p, which).wait_recv()
+        send_half(p).wait_send()
+        send_other(p).wait_send()
+        each_peer(lambda d: send_slot(p, d).wait_send())
+        each_peer(lambda d: send_back(p, d).wait_send())
     each_peer(lambda d: send_stat(d).wait_send())
     send_stat_rep(0, pair).wait_send()
     send_stat_rep(1, half).wait_send()
 
 
 CHUNKS = 8
+LAG = 4
 
 
 def local(grad_parts, params, accum, left_pre, right_pre, slot_block, layer_of):
@@ -328,6 +373,7 @@
     assert lax.axis_size("rep") == 4 and left_pre.shape[2] == 1
     rb, rows, size = params.shape
     chunks = CHUNKS
+    more = chunks + 1
     width = size // chunks
     tile = 256
     any_space = pl.BlockSpec(memory_space=pl.ANY)
@@ -351,13 +397,13 @@
             vmem(twice, BF16), vmem(twice, BF16), vmem(part, BF16), vmem(part, BF16), vmem(part, BF16),
             vmem(slots, BF16), vmem(whole, BF16), vmem((size, size), BF16), vmem((size, size), BF16),
             vmem((size, size), F32), vmem(whole, BF16),
-            [vmem(slots[1:], BF16)] * chunks, vmem(part, BF16), vmem(part, BF16), vmem(part, BF16), vmem(part, F32),
+            [vmem((n, m, width), BF16) for m in [rows] * (chunks - 1) + [rows // 2] * 2], vmem(part, BF16), vmem(part, BF16), vmem(part, BF16), vmem(part, F32),
             vmem((rb, 8, width), F32), vmem((8, size), F32), vmem((rb, 1, width), F32),
             vmem((8, LANES), F32), vmem((n, 8, LANES), F32), vmem((4, 8, LANES), F32),
-            dma((5, chunks + 1)), dma((chunks, 2)), dma((chunks, 2)), dma((chunks,)), dma((chunks,)),
-            dma((chunks, n)), dma((chunks, n)), dma((chunks, n)), dma((chunks, n)),
-            dma((n,)), dma((n,)), dma((2,)), dma((2,)), dma((chunks,)), dma((chunks,)),
-            dma((chunks, 2)), dma((chunks, 2)), dma((3, chunks)),
+            dma((5, more)), dma((chunks, 2)), dma((chunks, 2)), dma((more,)), dma((more,)),
+            dma((more, n)), dma((more, n)), dma((more, n)), dma((more, n)),
+            dma((n,)), dma((n,)), dma((2,)), dma((2,)), dma((more,)), dma((more,)),
+            dma((more, 2)), dma((more, 2)), dma((3, more)),
             pltpu.SMEM((slot_block.shape[0], 1, n), jnp.int32), pltpu.SMEM(layer_of.shape, jnp.int32),
         ],
         compiler_params=pltpu.CompilerParams(

time: 134 us -> 135 us (level)
  no operation moved by 1% of the time
where the time goes in v3:
time: 135 us; the launch traced here: 134 us
  Pallas kernels  129 us (96%)
  local copies, waits for them, and re-layouts  4.37 us (3%)
    pallas_call x1, Pallas kernels, local(): pl.pallas_call(functools.partial(kernel, n, chunks, width, rb, rows, size...  129 us
    unnamed x2, local copies, waits for them, and re-layouts  4.37 us

profile of v3, /device:TPU:0, one launch (start us, length us, event | category | flops | bytes accessed | tf_op | source)
XLA Modules:
  0.0 134.4 jit_solution(4229414192974501479)
XLA Ops:
  0.6 129.4 %shard_map.86 = (bf16[24,128,1024]{2,1,0:T(8,128)(2,1)S(1)}, f32[6,128,1024]{2,1,0:T(8,128)S(1)}) custom-call(s32[4,1,8]{2,1,0:T(1,128)} %bitcast.3, s32[24]{0:T(128)} %layer_in.1, bf16[1,24,128,1024]{3,2,1,0:T(8,128)(2,1)} %grad.1, bf16[6,128,1024]{2,1,0:T(8,128)(2,1)} %params.1, f32[6,128,1024]{2,1,0:T(8,128)} %accum.1, ...), custom_call_target="tpu_custom_call" | custom-call | tf_op jit(solution)/shard_map/pallas_call | solution.py:388
  130.0 2.7 %copy.12 = bf16[24,128,1024]{2,1,0:T(8,128)(2,1)} copy(bf16[24,128,1024]{2,1,0:T(8,128)(2,1)S(1)} %get-tuple-element.4) | data formatting | bytes 12582912
  132.7 1.7 %copy.13 = f32[6,128,1024]{2,1,0:T(8,128)} copy(f32[6,128,1024]{2,1,0:T(8,128)S(1)} %get-tuple-element.5) | data formatting | bytes 6291456
